TPU v7x, 32 devices: a whole 2x2x4 slice. The times are simulated.
32 devices in a mesh: freq: 4 (over y, x), row: 8 (over z, core).
Axes of the slice: x: 2, y: 2, z: 4, core: 2. Of those that a mesh axis runs over, the one named last changes fastest.
Arguments:
- data: bfloat16 [4, 2, 2048, 2048], P('freq', None, 'row'), may hold values from -60 to 60
Outputs:
- solution: float32 [4, 2, 2048, 2048], P('freq', None, 'row')
- direction: float32 [4, 2, 2048, 2048], P('freq', None, 'row')
All inputs are finite; a program needn't handle non-finite values.
Results may differ from a plain program's by a relative error of at most 0.0042.
Values may be sent and summed in bfloat16 or wider, within the bound.
A program may use at most 128 MiB of HBM per device.

v0:
```python
import jax
import jax.numpy as jnp
from jax import lax
from jax.sharding import PartitionSpec as P

ITERS = 2


def times_data(rounded, block):
    real_part = jnp.einsum(
        "frk,fkn->frn", rounded[:, 0], block[:, 0], preferred_element_type=jnp.float32
    ) - jnp.einsum("frk,fkn->frn", rounded[:, 1], block[:, 1], preferred_element_type=jnp.float32)
    imag_part = jnp.einsum(
        "frk,fkn->frn", rounded[:, 0], block[:, 1], preferred_element_type=jnp.float32
    ) + jnp.einsum("frk,fkn->frn", rounded[:, 1], block[:, 0], preferred_element_type=jnp.float32)
    return jnp.stack([real_part, imag_part], axis=1)


def times_adjoint(rounded, block):
    real_part = jnp.einsum(
        "frk,fnk->frn", rounded[:, 0], block[:, 0], preferred_element_type=jnp.float32
    ) + jnp.einsum("frk,fnk->frn", rounded[:, 1], block[:, 1], preferred_element_type=jnp.float32)
    imag_part = jnp.einsum(
        "frk,fnk->frn", rounded[:, 1], block[:, 0], preferred_element_type=jnp.float32
    ) - jnp.einsum("frk,fnk->frn", rounded[:, 0], block[:, 1], preferred_element_type=jnp.float32)
    return jnp.stack([real_part, imag_part], axis=1)


def on_device(data):
    order = data.shape[3]
    weight = 1.0 / (3.0 * (2.0 * order) ** 0.5)
    observed = data.astype(jnp.float32)
    zeros = jnp.zeros_like(observed)
    whole = lax.all_gather(data, "row", axis=2, tiled=True)
    first_image = observed - weight * times_adjoint(observed.astype(jnp.bfloat16), whole)

    def pair_step(data_raw, model_unit, image):
        data_sq, image_sq, cross, model_sq = lax.psum(
            (
                jnp.sum(data_raw * data_raw),
                jnp.sum(image * image),
                jnp.sum(image * model_unit),
                jnp.sum(model_unit * model_unit),
            ),
            ("freq", "row"),
        )
        beta_now = jnp.sqrt(data_sq)
        model_raw = image / beta_now - beta_now * model_unit
        alpha_now = jnp.sqrt(
            image_sq / (beta_now * beta_now) - 2.0 * cross + beta_now * beta_now * model_sq
        )
        return (beta_now, data_raw / beta_now, model_raw, alpha_now, model_raw / alpha_now)

    beta_now, data_unit, model_raw, alpha_now, model_unit = pair_step(observed, zeros, first_image)
    solution = zeros
    direction = model_unit
    phi_bar = beta_now
    rho_bar = alpha_now
    for iteration in range(ITERS):
        data_raw = (
            model_raw - weight * times_data(model_raw.astype(jnp.bfloat16), whole)
        ) / alpha_now - alpha_now * data_unit
        beta_now, data_unit, model_raw, alpha_now, model_unit = pair_step(
            data_raw,
            model_unit,
            data_raw - weight * times_adjoint(data_raw.astype(jnp.bfloat16), whole),
        )
        rho_value = jnp.sqrt(rho_bar * rho_bar + beta_now * beta_now)
        cosine = rho_bar / rho_value
        sine_value = beta_now / rho_value
        theta_value = sine_value * alpha_now
        rho_bar = -cosine * alpha_now
        phi_value = cosine * phi_bar
        phi_bar = sine_value * phi_bar
        solution = solution + phi_value / rho_value * direction
        direction = model_unit - theta_value / rho_value * direction
    return (solution, direction)


def solution(mesh):
    return jax.shard_map(
        on_device,
        mesh=mesh,
        in_specs=(P("freq", None, "row", None),),
        out_specs=(P("freq", None, "row", None), P("freq", None, "row", None)),
        check_vma=False,
    )
```

profile of v0, /device:TPU:12, one launch (start us, length us, event | category | flops | bytes accessed | tf_op | source)
XLA Modules:
  0.0 439.7 jit_solution(2059661497259600702)
XLA Ops:
  7.2 0.0 all-gather.2.cloned.1.call-start
  7.2 0.7 all-gather.2.cloned.1.call-update
  7.9 151.1 %all-gather.2.cloned.1.call-done = bf16[1,2,2048,2048]{3,2,1,0:T(8,128)(2,1)} async-done(((bf16[1,2,256,2048]{3,2,1,0:T(8,128)(2,1)}), bf16[1,2,2048,2048]{3,2,1,0:T(8,128)(2,1)}) %all-gather.2.cloned.1.call-update) | async-done | bytes 16777232 | tf_op jit(solution)/shard_map/all_gather | solution.py:34
  159.1 6.2 %fusion.20 = f32[256,2048]{1,0:T(8,128)S(1)} fusion(bf16[1,2,256,2048]{3,2,1,0:T(8,128)(2,1)} %param.1, bf16[1,2,2048,2048]{3,2,1,0:T(8,128)(2,1)} %all-gather.2.cloned.1.call-done), kind=kOutput, calls=%fused_computation.65 | convolution fusion | flops 2147483648 | bytes 11534336 | tf_op jit(solution)/shard_map/frk,fnk->frn/dot_general | solution.py:23
  165.3 0.0 slice-start.2
  165.3 0.0 slice-start.3
  165.3 5.9 %fusion.24 = f32[256,2048]{1,0:T(8,128)S(1)} fusion(bf16[1,2,256,2048]{3,2,1,0:T(8,128)(2,1)S(1)} %copy-done.3, bf16[1,2,2048,2048]{3,2,1,0:T(8,128)(2,1)} %all-gather.2.cloned.1.call-done), kind=kOutput, calls=%fused_computation.69 | convolution fusion | flops 2147483648 | bytes 11534336 | tf_op jit(solution)/shard_map/frk,fnk->frn/dot_general | solution.py:20
  171.2 2.4 fusion.18
  173.6 0.0 copy-start.5
  173.6 2.4 fusion.19
  176.0 0.0 copy-start.7
  176.0 1.9 multiply_reduce_fusion.8
  178.0 44.0 %all-reduce.2 = (f32[]{:T(128)}, f32[]{:T(128)}, f32[]{:T(128)}, f32[]{:T(128)}) all-reduce(f32[]{:T(128)} %get-tuple-element.7, f32[]{:T(128)} %get-tuple-element.12, f32[]{:T(128)} %get-tuple-element.6, f32[]{:T(128)} %constant.2.clone.1), channel_id=1, replica_groups=mesh['freq'=4,'row'=8] {'freq','row'}, use_global_device_ids=true, to_apply=%region_1.0 | all-reduce | flops 4 | bytes 32 | tf_op jit(solution)/shard_map/psum | solution.py:38
  224.6 4.4 %fusion.38 = bf16[1,2,256,2048]{3,2,1,0:T(8,128)(2,1)} fusion(f32[]{:T(128)S(6)} %mul.197, f32[]{:T(128)S(6)} %sqrt.24, f32[1,1,256,2048]{3,2,1,0:T(8,128)} %copy-done.5, f32[1,1,256,2048]{3,2,1,0:T(8,128)} %copy-done.7, bf16[1,2,256,2048]{3,2,1,0:T(8,128)(2,1)S(1)} %copy-done.3), kind=kLoop, calls=%fused_computation.83 | loop fusion | flops 7340032 | bytes 8388616 | tf_op jit(solution)/shard_map/convert_element_type | solution.py:61
  229.0 6.2 %fusion.26 = f32[256,2048]{1,0:T(8,128)S(1)} fusion(bf16[1,2,256,2048]{3,2,1,0:T(8,128)(2,1)} %fusion.38, bf16[1,2,2048,2048]{3,2,1,0:T(8,128)(2,1)} %all-gather.2.cloned.1.call-done), kind=kOutput, calls=%fused_computation.71 | convolution fusion | flops 2147483648 | bytes 11534336 | tf_op jit(solution)/shard_map/frk,fkn->frn/dot_general | solution.py:13
  235.2 5.7 %fusion.27 = f32[256,2048]{1,0:T(8,128)S(1)} fusion(bf16[1,2,256,2048]{3,2,1,0:T(8,128)(2,1)S(1)} %copy-done.12, bf16[1,2,2048,2048]{3,2,1,0:T(8,128)(2,1)} %all-gather.2.cloned.1.call-done), kind=kOutput, calls=%fused_computation.72 | convolution fusion | flops 2147483648 | bytes 11534336 | tf_op jit(solution)/shard_map/frk,fkn->frn/dot_general | solution.py:10
  240.9 5.8 %fusion.16 = f32[1,1,256,2048]{3,2,1,0:T(8,128)S(1)} fusion(f32[256,2048]{1,0:T(8,128)S(1)} %fusion.26, bf16[1,2,256,2048]{3,2,1,0:T(8,128)(2,1)S(1)} %copy-done.12, bf16[1,2,2048,2048]{3,2,1,0:T(8,128)(2,1)} %all-gather.2.cloned.1.call-done), kind=kOutput, calls=%fused_computation.48 | convolution fusion | flops 2148007936 | bytes 13631488 | tf_op jit(solution)/shard_map/frk,fkn->frn/dot_general | solution.py:15
  246.7 0.0 copy-start.6
  246.7 0.0 copy-start.8
  246.7 5.9 %fusion.17 = f32[1,1,256,2048]{3,2,1,0:T(8,128)S(1)} fusion(f32[256,2048]{1,0:T(8,128)S(1)} %fusion.27, bf16[1,2,256,2048]{3,2,1,0:T(8,128)(2,1)S(1)} %copy-done.12, bf16[1,2,2048,2048]{3,2,1,0:T(8,128)(2,1)} %all-gather.2.cloned.1.call-done), kind=kOutput, calls=%fused_computation.50 | convolution fusion | flops 2148007936 | bytes 13631488 | tf_op jit(solution)/shard_map/frk,fkn->frn/dot_general | solution.py:12
  252.7 1.9 fusion.42
  254.6 0.0 copy-start
  254.6 7.3 %fusion.29 = f32[256,2048]{1,0:T(8,128)S(1)} fusion(bf16[1,2,256,2048]{3,2,1,0:T(8,128)(2,1)S(1)} %get-tuple-element.30, bf16[1,2,2048,2048]{3,2,1,0:T(8,128)(2,1)} %all-gather.2.cloned.1.call-done), kind=kOutput, calls=%fused_computation.74 | convolution fusion | flops 2147483648 | bytes 11534336 | tf_op jit(solution)/shard_map/frk,fnk->frn/dot_general | solution.py:23
  261.9 5.7 %fusion.28 = f32[256,2048]{1,0:T(8,128)S(1)} fusion(bf16[1,2,256,2048]{3,2,1,0:T(8,128)(2,1)S(1)} %get-tuple-element.30, bf16[1,2,2048,2048]{3,2,1,0:T(8,128)(2,1)} %all-gather.2.cloned.1.call-done), kind=kOutput, calls=%fused_computation.73 | convolution fusion | flops 2147483648 | bytes 11534336 | tf_op jit(solution)/shard_map/frk,fnk->frn/dot_general | solution.py:20
  267.6 5.7 %fusion.14 = f32[1,1,256,2048]{3,2,1,0:T(8,128)S(1)} fusion(f32[256,2048]{1,0:T(8,128)S(1)} %fusion.29, bf16[1,2,256,2048]{3,2,1,0:T(8,128)(2,1)S(1)} %get-tuple-element.30, bf16[1,2,2048,2048]{3,2,1,0:T(8,128)(2,1)} %all-gather.2.cloned.1.call-done), kind=kOutput, calls=%fused_computation.44 | convolution fusion | flops 2148007936 | bytes 13631488 | tf_op jit(solution)/shard_map/frk,fnk->frn/dot_general | solution.py:25
  273.4 6.5 %fusion.15 = f32[1,1,256,2048]{3,2,1,0:T(8,128)S(1)} fusion(f32[256,2048]{1,0:T(8,128)S(1)} %fusion.28, bf16[1,2,256,2048]{3,2,1,0:T(8,128)(2,1)S(1)} %get-tuple-element.30, bf16[1,2,2048,2048]{3,2,1,0:T(8,128)(2,1)} %all-gather.2.cloned.1.call-done), kind=kOutput, calls=%fused_computation.46 | convolution fusion | flops 2148007936 | bytes 13631488 | tf_op jit(solution)/shard_map/frk,fnk->frn/dot_general | solution.py:22
  279.9 0.0 copy-start.11
  279.9 4.2 multiply_reduce_fusion.5
  284.1 39.4 %all-reduce.1 = (f32[]{:T(128)}, f32[]{:T(128)}, f32[]{:T(128)}, f32[]{:T(128)}) all-reduce(f32[]{:T(128)} %get-tuple-element.11, f32[]{:T(128)} %get-tuple-element.5, f32[]{:T(128)} %get-tuple-element.4, f32[]{:T(128)} %get-tuple-element.10), channel_id=1, replica_groups=mesh['freq'=4,'row'=8] {'freq','row'}, use_global_device_ids=true, to_apply=%region_8.0 | all-reduce | flops 4 | bytes 32 | tf_op jit(solution)/shard_map/psum | solution.py:38
  326.2 0.0 slice-start.4
  326.2 0.0 slice-start.5
  326.2 0.0 slice-start.6
  326.2 5.5 %fusion.41 = (bf16[1,2,256,2048]{3,2,1,0:T(8,128)(2,1)S(1)}, f32[1,2,256,2048]{3,2,1,0:T(8,128)S(1)}) fusion(f32[1,2,256,2048]{3,2,1,0:T(8,128)} %get-tuple-element.29, f32[]{:T(128)S(6)} %sqrt.26, f32[1,2,256,2048]{3,2,1,0:T(8,128)} %copy-done, f32[1,1,256,2048]{3,2,1,0:T(8,128)} %copy-done.10, f32[1,1,256,2048]{3,2,1,0:T(8,128)} %copy-done.11), kind=kLoop, calls=%fused_computation.85 | loop fusion | flops 7340032 | bytes 18874372 | tf_op jit(solution)/shard_map/convert_element_type | solution.py:61
  331.7 0.0 slice-start.7
  331.7 8.1 %fusion.30 = f32[256,2048]{1,0:T(8,128)S(1)} fusion(bf16[1,2,256,2048]{3,2,1,0:T(8,128)(2,1)S(1)} %get-tuple-element.27, bf16[1,2,2048,2048]{3,2,1,0:T(8,128)(2,1)} %all-gather.2.cloned.1.call-done), kind=kOutput, calls=%fused_computation.75 | convolution fusion | flops 2147483648 | bytes 11534336 | tf_op jit(solution)/shard_map/frk,fkn->frn/dot_general | solution.py:13
  339.8 2.3 fusion.31
  342.2 2.4 fusion.12
  344.6 0.0 copy-start.1
  344.6 5.9 %fusion.13 = f32[1,1,256,2048]{3,2,1,0:T(8,128)S(1)} fusion(f32[256,2048]{1,0:T(8,128)S(1)} %fusion.31, bf16[1,2,256,2048]{3,2,1,0:T(8,128)(2,1)S(1)} %get-tuple-element.27, bf16[1,2,2048,2048]{3,2,1,0:T(8,128)(2,1)} %all-gather.2.cloned.1.call-done), kind=kOutput, calls=%fused_computation.42 | convolution fusion | flops 2148007936 | bytes 13631488 | tf_op jit(solution)/shard_map/frk,fkn->frn/dot_general | solution.py:12
  350.5 1.6 fusion.39
  352.1 0.0 copy-start.4
  352.1 7.3 %fusion.33 = f32[256,2048]{1,0:T(8,128)S(1)} fusion(bf16[1,2,256,2048]{3,2,1,0:T(8,128)(2,1)S(1)} %get-tuple-element.25, bf16[1,2,2048,2048]{3,2,1,0:T(8,128)(2,1)} %all-gather.2.cloned.1.call-done), kind=kOutput, calls=%fused_computation.78 | convolution fusion | flops 2147483648 | bytes 11534336 | tf_op jit(solution)/shard_map/frk,fnk->frn/dot_general | solution.py:23
  359.4 5.7 %fusion.32 = f32[256,2048]{1,0:T(8,128)S(1)} fusion(bf16[1,2,256,2048]{3,2,1,0:T(8,128)(2,1)S(1)} %get-tuple-element.25, bf16[1,2,2048,2048]{3,2,1,0:T(8,128)(2,1)} %all-gather.2.cloned.1.call-done), kind=kOutput, calls=%fused_computation.77 | convolution fusion | flops 2147483648 | bytes 11534336 | tf_op jit(solution)/shard_map/frk,fnk->frn/dot_general | solution.py:20
  365.2 5.7 %fusion.10 = f32[1,1,256,2048]{3,2,1,0:T(8,128)S(1)} fusion(f32[256,2048]{1,0:T(8,128)S(1)} %fusion.33, bf16[1,2,256,2048]{3,2,1,0:T(8,128)(2,1)S(1)} %get-tuple-element.25, bf16[1,2,2048,2048]{3,2,1,0:T(8,128)(2,1)} %all-gather.2.cloned.1.call-done), kind=kOutput, calls=%fused_computation.36 | convolution fusion | flops 2148007936 | bytes 13631488 | tf_op jit(solution)/shard_map/frk,fnk->frn/dot_general | solution.py:25
  370.9 5.7 %fusion.11 = f32[1,1,256,2048]{3,2,1,0:T(8,128)S(1)} fusion(f32[256,2048]{1,0:T(8,128)S(1)} %fusion.32, bf16[1,2,256,2048]{3,2,1,0:T(8,128)(2,1)S(1)} %get-tuple-element.25, bf16[1,2,2048,2048]{3,2,1,0:T(8,128)(2,1)} %all-gather.2.cloned.1.call-done), kind=kOutput, calls=%fused_computation.38 | convolution fusion | flops 2148007936 | bytes 13631488 | tf_op jit(solution)/shard_map/frk,fnk->frn/dot_general | solution.py:22
  376.7 2.2 multiply_reduce_fusion.1
  378.9 42.1 %all-reduce = (f32[]{:T(128)}, f32[]{:T(128)}, f32[]{:T(128)}, f32[]{:T(128)}) all-reduce(f32[]{:T(128)} %get-tuple-element.9, f32[]{:T(128)} %get-tuple-element.3, f32[]{:T(128)} %get-tuple-element.2, f32[]{:T(128)} %get-tuple-element.8), channel_id=1, replica_groups=mesh['freq'=4,'row'=8] {'freq','row'}, use_global_device_ids=true, to_apply=%region_16.0 | all-reduce | flops 4 | bytes 32 | tf_op jit(solution)/shard_map/psum | solution.py:38
  424.0 8.7 %multiply_subtract_fusion = (f32[1,2,256,2048]{3,2,1,0:T(8,128)}, f32[1,2,256,2048]{3,2,1,0:T(8,128)}) fusion(f32[1,2,256,2048]{3,2,1,0:T(8,128)} %get-tuple-element.29, f32[]{:T(128)S(6)} %div.111, f32[]{:T(128)S(6)} %sqrt.31, f32[]{:T(128)S(6)} %sqrt.29, f32[]{:T(128)S(6)} %div.104, f32[1,2,256,2048]{3,2,1,0:T(8,128)} %copy-done.4, ...), kind=kLoop, calls=%fused_computation.20 | loop fusion | flops 15728640 | bytes 25165852 | tf_op jit(solution)/shard_map/sub | solution.py:76
  (30 shorter events, 0.1 us)
Async XLA Ops:
  7.2 151.9 %all-gather.2.cloned.1.call-start = ((), (), s32[]{:S(2)}) async-start(), calls=%async_computation | async-start | bytes 18874368 | tf_op jit(solution)/shard_map/all_gather | solution.py:34
  7.9 157.4 %copy-start.3 = (bf16[1,2,256,2048]{3,2,1,0:T(8,128)(2,1)S(1)}, bf16[1,2,256,2048]{3,2,1,0:T(8,128)(2,1)}, u32[]{:S(2)}) copy-start(bf16[1,2,256,2048]{3,2,1,0:T(8,128)(2,1)} %param.1) | copy-start | bytes 6291460
  159.1 12.1 %slice-start = ((s8[16777216]{0:T(1024)(128)(4,1)}), s8[4194304]{0:T(1024)(128)(4,1)S(1)}, s32[]{:S(2)}) async-start(s8[16777216]{0:T(1024)(128)(4,1)} %bitcast.86), calls=%async_computation.1 | async-start | bytes 8388608
  159.1 12.2 %slice-start.1 = ((s8[16777216]{0:T(1024)(128)(4,1)}), s8[4194304]{0:T(1024)(128)(4,1)S(1)}, s32[]{:S(2)}) async-start(s8[16777216]{0:T(1024)(128)(4,1)} %bitcast.86), calls=%async_computation.2 | async-start | bytes 8388608
  165.3 5.9 %slice-start.2 = ((s8[16777216]{0:T(1024)(128)(4,1)}), s8[4194304]{0:T(1024)(128)(4,1)S(1)}, s32[]{:S(2)}) async-start(s8[16777216]{0:T(1024)(128)(4,1)} %bitcast.86), calls=%async_computation.3 | async-start | bytes 8388608
  165.3 5.9 %slice-start.3 = ((s8[16777216]{0:T(1024)(128)(4,1)}), s8[4194304]{0:T(1024)(128)(4,1)S(1)}, s32[]{:S(2)}) async-start(s8[16777216]{0:T(1024)(128)(4,1)} %bitcast.86), calls=%async_computation.4 | async-start | bytes 8388608
  173.6 2.4 copy-start.5
  176.0 1.9 copy-start.7
  229.0 6.2 %copy-start.12 = (bf16[1,2,256,2048]{3,2,1,0:T(8,128)(2,1)S(1)}, bf16[1,2,256,2048]{3,2,1,0:T(8,128)(2,1)}, u32[]{:S(2)}) copy-start(bf16[1,2,256,2048]{3,2,1,0:T(8,128)(2,1)} %fusion.38) | copy-start | bytes 6291460
  246.7 6.0 %copy-start.6 = (f32[1,1,256,2048]{3,2,1,0:T(8,128)S(1)}, f32[1,1,256,2048]{3,2,1,0:T(8,128)}, u32[]{:S(2)}) copy-start(f32[1,1,256,2048]{3,2,1,0:T(8,128)} %copy-done.5) | copy-start | bytes 6291460
  246.7 6.0 %copy-start.8 = (f32[1,1,256,2048]{3,2,1,0:T(8,128)S(1)}, f32[1,1,256,2048]{3,2,1,0:T(8,128)}, u32[]{:S(2)}) copy-start(f32[1,1,256,2048]{3,2,1,0:T(8,128)} %copy-done.7) | copy-start | bytes 6291460
  254.6 25.3 %copy-start = (f32[1,2,256,2048]{3,2,1,0:T(8,128)}, f32[1,2,256,2048]{3,2,1,0:T(8,128)S(1)}, u32[]{:S(2)}) copy-start(f32[1,2,256,2048]{3,2,1,0:T(8,128)S(1)} %get-tuple-element.31) | copy-start | bytes 12582916
  273.4 6.5 %copy-start.10 = (f32[1,1,256,2048]{3,2,1,0:T(8,128)}, f32[1,1,256,2048]{3,2,1,0:T(8,128)S(1)}, u32[]{:S(2)}) copy-start(f32[1,1,256,2048]{3,2,1,0:T(8,128)S(1)} %fusion.14) | copy-start | bytes 6291460
  279.9 4.3 copy-start.11
  326.2 13.6 %slice-start.4 = ((s8[16777216]{0:T(1024)(128)(4,1)}), s8[4194304]{0:T(1024)(128)(4,1)S(1)}, s32[]{:S(2)}) async-start(s8[16777216]{0:T(1024)(128)(4,1)} %bitcast.88), calls=%async_computation.5 | async-start | bytes 8388608
  326.2 13.6 %slice-start.5 = ((s8[16777216]{0:T(1024)(128)(4,1)}), s8[4194304]{0:T(1024)(128)(4,1)S(1)}, s32[]{:S(2)}) async-start(s8[16777216]{0:T(1024)(128)(4,1)} %bitcast.88), calls=%async_computation.6 | async-start | bytes 8388608
  326.2 13.6 %slice-start.6 = ((s8[16777216]{0:T(1024)(128)(4,1)}), s8[4194304]{0:T(1024)(128)(4,1)S(1)}, s32[]{:S(2)}) async-start(s8[16777216]{0:T(1024)(128)(4,1)} %bitcast.88), calls=%async_computation.7 | async-start | bytes 8388608
  331.7 45.0 %copy-start.2 = (f32[1,2,256,2048]{3,2,1,0:T(8,128)}, f32[1,2,256,2048]{3,2,1,0:T(8,128)S(1)}, u32[]{:S(2)}) copy-start(f32[1,2,256,2048]{3,2,1,0:T(8,128)S(1)} %get-tuple-element.28) | copy-start | bytes 12582916
  331.7 8.1 %slice-start.7 = ((s8[16777216]{0:T(1024)(128)(4,1)}), s8[4194304]{0:T(1024)(128)(4,1)S(1)}, s32[]{:S(2)}) async-start(s8[16777216]{0:T(1024)(128)(4,1)} %bitcast.88), calls=%async_computation.8 | async-start | bytes 8388608
  344.6 5.9 %copy-start.1 = (f32[1,2,256,2048]{3,2,1,0:T(8,128)S(1)}, f32[1,2,256,2048]{3,2,1,0:T(8,128)}, u32[]{:S(2)}) copy-start(f32[1,2,256,2048]{3,2,1,0:T(8,128)} %copy-done) | copy-start | bytes 12582916
  352.1 24.5 %copy-start.4 = (f32[1,2,256,2048]{3,2,1,0:T(8,128)}, f32[1,2,256,2048]{3,2,1,0:T(8,128)S(1)}, u32[]{:S(2)}) copy-start(f32[1,2,256,2048]{3,2,1,0:T(8,128)S(1)} %get-tuple-element.26) | copy-start | bytes 12582916
  376.7 2.2 copy-start.9
Sparse Core Ops, SparseCore 0:
  9.6 149.4 all-gather.1
where the time goes:
time: 447 us; the launch traced here: 440 us
  waiting for transfers between devices  152 us (34%)
  blocking collectives  126 us (28%)
  matrix products  109 us (24%)
  other arithmetic  30.5 us (7%)
  between operations  22.8 us (5%)
    all_gather x1, waiting for transfers between devices, on_device(): whole = lax.all_gather(data, 'row', axis=2, tiled=True)  151 us
    psum x3, blocking collectives, pair_step(): lax.psum((jnp.sum(data_raw * data_raw), jnp.sum(image * image), jnp.sum(i...  126 us
    dot_general x3, matrix products, times_adjoint(): jnp.einsum('frk,fnk->frn', rounded[:, 1], block[:, 0], preferred_element_...  20.7 us
    dot_general x3, matrix products, times_adjoint(): jnp.einsum('frk,fnk->frn', rounded[:, 0], block[:, 0], preferred_element_...  17.4 us
    dot_general x3, matrix products, times_adjoint(): jnp.einsum('frk,fnk->frn', rounded[:, 1], block[:, 1], preferred_element_...  14.6 us
    dot_general x2, matrix products, times_data(): jnp.einsum('frk,fkn->frn', rounded[:, 0], block[:, 1], preferred_element_...  14.2 us
    dot_general x3, matrix products, times_adjoint(): jnp.einsum('frk,fnk->frn', rounded[:, 0], block[:, 1], preferred_element_...  13.9 us
    dot_general x2, matrix products, times_data(): jnp.einsum('frk,fkn->frn', rounded[:, 1], block[:, 1], preferred_element_...  11.8 us
  transfers between devices with their start and end apart: 1, of which 1 were waited for; matrix products, arithmetic and copies ran while one was open for 0% of the time, Pallas kernels for 0%

commit v1 on v0

--- a/solution.py
+++ b/solution.py
@@ -4,6 +4,18 @@
 from jax.sharding import PartitionSpec as P
 
 ITERS = 2
+
+
+def fill_halves_on_mesh(block_here, row_dim):
+    lanes = jax.lax.axis_size("row")
+    y = block_here
+    history = [y]
+    e_next = sorted(((k, (k + 1) % lanes) for k in range(lanes)))
+    for j0 in [*range(1, lanes)]:
+        y = jax.lax.ppermute(y, axis_name="row", perm=e_next)
+        history.insert(0, y)
+    m_next = jnp.concatenate(history, row_dim)
+    return jnp.roll(m_next, (jax.lax.axis_index("row") + 1) * block_here.shape[row_dim], row_dim)
 
 
 def times_data(rounded, block):
@@ -31,7 +43,7 @@
     weight = 1.0 / (3.0 * (2.0 * order) ** 0.5)
     observed = data.astype(jnp.float32)
     zeros = jnp.zeros_like(observed)
-    whole = lax.all_gather(data, "row", axis=2, tiled=True)
+    whole = fill_halves_on_mesh(data, row_dim=2)
     first_image = observed - weight * times_adjoint(observed.astype(jnp.bfloat16), whole)
 
     def pair_step(data_raw, model_unit, image):

time: 447 us -> 555 us (1.24)
  local copies, waits for them, and re-layouts: 0.1 us -> 51.8 us
  matrix products: 109 us -> 141 us
  waiting for transfers between devices: 152 us -> 176 us
  between operations: 22.8 us -> 9.72 us
  blocking collectives: 126 us -> 135 us
    ppermute x0 -> x7, waiting for transfers between devices: none -> 176 us  [fill_halves_on_mesh(): y = jax.lax.ppermute(y, axis_name='row', perm=e_next)]
    all_gather x1 -> x0, waiting for transfers between devices: 151 us -> none  [on_device(): whole = lax.all_gather(data, 'row', axis=2, tiled=True)]
    unnamed x42 -> x78, local copies, waits for them, and re-layouts: 0.1 us -> 50.3 us
    psum x3, blocking collectives: 126 us -> 135 us  [pair_step(): lax.psum((jnp.sum(data_raw * data_raw), jnp.sum(image * image), jnp.sum(i...]
    dot_general x2, matrix products: 8.19 us -> 16.9 us  [times_data(): jnp.einsum('frk,fkn->frn', rounded[:, 1], block[:, 0], preferred_element_...]
    dot_general x3, matrix products: 13.9 us -> 21 us  [times_adjoint(): jnp.einsum('frk,fnk->frn', rounded[:, 0], block[:, 1], preferred_element_...]
    dot_general x2, matrix products: 8.06 us -> 14.5 us  [times_data(): jnp.einsum('frk,fkn->frn', rounded[:, 0], block[:, 0], preferred_element_...]
  transfers between devices with their start and end apart: 1 -> 7, of which waited for: 1 -> 7; matrix products, arithmetic and copies ran while one was open for 0% -> 1% of each run, Pallas kernels for 0% -> 0%
where the time goes in v1:
time: 555 us; the launch traced here: 545 us
  waiting for transfers between devices  176 us (32%)
  matrix products  141 us (25%)
  blocking collectives  135 us (24%)
  local copies, waits for them, and re-layouts  51.8 us (9%)
  other arithmetic  32 us (6%)
  between operations  9.72 us (2%)
    ppermute x7, waiting for transfers between devices, fill_halves_on_mesh(): y = jax.lax.ppermute(y, axis_name='row', perm=e_next)  176 us
    psum x3, blocking collectives, pair_step(): lax.psum((jnp.sum(data_raw * data_raw), jnp.sum(image * image), jnp.sum(i...  135 us
    unnamed x78, local copies, waits for them, and re-layouts  50.3 us
    dot_general x3, matrix products, times_adjoint(): jnp.einsum('frk,fnk->frn', rounded[:, 0], block[:, 1], preferred_element_...  21 us
    dot_general x3, matrix products, times_adjoint(): jnp.einsum('frk,fnk->frn', rounded[:, 0], block[:, 0], preferred_element_...  19.4 us
    dot_general x3, matrix products, times_adjoint(): jnp.einsum('frk,fnk->frn', rounded[:, 1], block[:, 0], preferred_element_...  18.7 us
    dot_general x3, matrix products, times_adjoint(): jnp.einsum('frk,fnk->frn', rounded[:, 1], block[:, 1], preferred_element_...  18.7 us
    dot_general x2, matrix products, times_data(): jnp.einsum('frk,fkn->frn', rounded[:, 1], block[:, 0], preferred_element_...  16.9 us
  transfers between devices with their start and end apart: 7, of which 7 were waited for; matrix products, arithmetic and copies ran while one was open for 1% of the time, Pallas kernels for 0%

profile of v1, /device:TPU:12, one launch (start us, length us, event | category | flops | bytes accessed | tf_op | source)
XLA Modules:
  0.0 544.6 jit_solution(952164531706060128)
XLA Ops:
  0.7 25.7 %collective-permute-done = bf16[1,2,256,2048]{3,2,1,0:T(8,128)(2,1)S(1)} collective-permute-done((bf16[1,2,256,2048]{3,2,1,0:T(8,128)(2,1)}, bf16[1,2,256,2048]{3,2,1,0:T(8,128)(2,1)S(1)}, u32[]{:S(2)}, u32[]{:S(2)}) %collective-permute-start) | collective-permute-done | bytes 2097184 | tf_op jit(solution)/shard_map/ppermute | solution.py:15
  27.7 25.5 %collective-permute-done.1 = bf16[1,2,256,2048]{3,2,1,0:T(8,128)(2,1)S(1)} collective-permute-done((bf16[1,2,256,2048]{3,2,1,0:T(8,128)(2,1)S(1)}, bf16[1,2,256,2048]{3,2,1,0:T(8,128)(2,1)S(1)}, u32[]{:S(2)}, u32[]{:S(2)}) %collective-permute-start.1) | collective-permute-done | bytes 2097184 | tf_op jit(solution)/shard_map/ppermute | solution.py:15
  54.4 25.5 %collective-permute-done.2 = bf16[1,2,256,2048]{3,2,1,0:T(8,128)(2,1)S(1)} collective-permute-done((bf16[1,2,256,2048]{3,2,1,0:T(8,128)(2,1)S(1)}, bf16[1,2,256,2048]{3,2,1,0:T(8,128)(2,1)S(1)}, u32[]{:S(2)}, u32[]{:S(2)}) %collective-permute-start.2) | collective-permute-done | bytes 2097184 | tf_op jit(solution)/shard_map/ppermute | solution.py:15
  81.2 25.5 %collective-permute-done.3 = bf16[1,2,256,2048]{3,2,1,0:T(8,128)(2,1)S(1)} collective-permute-done((bf16[1,2,256,2048]{3,2,1,0:T(8,128)(2,1)S(1)}, bf16[1,2,256,2048]{3,2,1,0:T(8,128)(2,1)S(1)}, u32[]{:S(2)}, u32[]{:S(2)}) %collective-permute-start.3) | collective-permute-done | bytes 2097184 | tf_op jit(solution)/shard_map/ppermute | solution.py:15
  108.0 25.5 %collective-permute-done.4 = bf16[1,2,256,2048]{3,2,1,0:T(8,128)(2,1)S(1)} collective-permute-done((bf16[1,2,256,2048]{3,2,1,0:T(8,128)(2,1)S(1)}, bf16[1,2,256,2048]{3,2,1,0:T(8,128)(2,1)S(1)}, u32[]{:S(2)}, u32[]{:S(2)}) %collective-permute-start.4) | collective-permute-done | bytes 2097184 | tf_op jit(solution)/shard_map/ppermute | solution.py:15
  134.8 25.6 %collective-permute-done.5 = bf16[1,2,256,2048]{3,2,1,0:T(8,128)(2,1)} collective-permute-done((bf16[1,2,256,2048]{3,2,1,0:T(8,128)(2,1)S(1)}, bf16[1,2,256,2048]{3,2,1,0:T(8,128)(2,1)}, u32[]{:S(2)}, u32[]{:S(2)}) %collective-permute-start.5) | collective-permute-done | bytes 2097184 | tf_op jit(solution)/shard_map/ppermute | solution.py:15
  160.4 2.8 copy.3
  163.2 22.9 %collective-permute-done.6 = bf16[1,2,256,2048]{3,2,1,0:T(8,128)(2,1)} collective-permute-done((bf16[1,2,256,2048]{3,2,1,0:T(8,128)(2,1)}, bf16[1,2,256,2048]{3,2,1,0:T(8,128)(2,1)}, u32[]{:S(2)}, u32[]{:S(2)}) %collective-permute-start.6) | collective-permute-done | bytes 2097184 | tf_op jit(solution)/shard_map/ppermute | solution.py:15
  186.1 3.2 constant_dynamic-update-slice_fusion.15
  189.3 3.5 constant_dynamic-update-slice_fusion.14
  197.4 1.6 constant_dynamic-update-slice_fusion.10
  200.5 1.5 constant_dynamic-update-slice_fusion.8
  202.0 3.3 constant_dynamic-update-slice_fusion.7
  205.3 3.2 constant_dynamic-update-slice_fusion.6
  211.5 1.6 constant_dynamic-update-slice_fusion.3
  217.7 5.9 %fusion.23 = f32[2048,256]{1,0:T(8,128)S(1)} fusion(bf16[1,2,256,2048]{3,2,1,0:T(8,128)(2,1)S(1)} %copy-done.9, bf16[1,2,4096,2048]{3,2,1,0:T(8,128)(2,1)} %constant_dynamic-update-slice_fusion, s32[]{:T(128)S(6)} %add.94, s32[]{:T(128)S(6)} %select_n.14), kind=kOutput, calls=%fused_computation.68 | convolution fusion | flops 2147483648 | bytes 11534344 | tf_op jit(solution)/shard_map/frk,fnk->frn/dot_general | solution.py:37
  223.6 5.9 %fusion.21 = f32[2048,256]{1,0:T(8,128)S(1)} fusion(bf16[1,2,256,2048]{3,2,1,0:T(8,128)(2,1)S(1)} %copy-done.9, bf16[1,2,4096,2048]{3,2,1,0:T(8,128)(2,1)} %constant_dynamic-update-slice_fusion, s32[]{:T(128)S(6)} %add.94, s32[]{:T(128)S(6)} %select_n.14), kind=kOutput, calls=%fused_computation.66 | convolution fusion | flops 2147483648 | bytes 11534344 | tf_op jit(solution)/shard_map/frk,fnk->frn/dot_general | solution.py:34
  229.5 6.0 %fusion.18 = f32[1,1,256,2048]{2,3,1,0:T(8,128)S(1)} fusion(f32[2048,256]{1,0:T(8,128)S(1)} %fusion.23, bf16[1,2,256,2048]{3,2,1,0:T(8,128)(2,1)S(1)} %copy-done.9, bf16[1,2,4096,2048]{3,2,1,0:T(8,128)(2,1)} %constant_dynamic-update-slice_fusion, s32[]{:T(128)S(6)} %select_n.14), kind=kOutput, calls=%fused_computation.52 | convolution fusion | flops 2148007936 | bytes 13631492 | tf_op jit(solution)/shard_map/frk,fnk->frn/dot_general | solution.py:35
  235.5 6.8 %fusion.19 = f32[1,1,256,2048]{2,3,1,0:T(8,128)S(1)} fusion(f32[2048,256]{1,0:T(8,128)S(1)} %fusion.21, bf16[1,2,256,2048]{3,2,1,0:T(8,128)(2,1)S(1)} %copy-done.9, bf16[1,2,4096,2048]{3,2,1,0:T(8,128)(2,1)} %constant_dynamic-update-slice_fusion, s32[]{:T(128)S(6)} %select_n.14), kind=kOutput, calls=%fused_computation.54 | convolution fusion | flops 2148007936 | bytes 13631492 | tf_op jit(solution)/shard_map/frk,fnk->frn/dot_general | solution.py:32
  242.3 2.1 multiply_reduce_fusion.8
  244.4 53.5 %all-reduce.2 = (f32[]{:T(128)}, f32[]{:T(128)}, f32[]{:T(128)}, f32[]{:T(128)}) all-reduce(f32[]{:T(128)} %get-tuple-element.9, f32[]{:T(128)} %get-tuple-element.14, f32[]{:T(128)} %get-tuple-element.8, f32[]{:T(128)} %constant.37.clone.1), channel_id=1, replica_groups=mesh['freq'=4,'row'=8] {'freq','row'}, use_global_device_ids=true, to_apply=%region_1.2 | all-reduce | flops 4 | bytes 32 | tf_op jit(solution)/shard_map/psum | solution.py:50
  298.7 3.0 fusion.38
  301.6 8.8 %fusion.26 = f32[256,2048]{0,1:T(8,128)} fusion(bf16[1,2,256,2048]{2,3,1,0:T(8,128)(2,1)S(1)} %fusion.38, bf16[1,2,4096,2048]{3,2,1,0:T(8,128)(2,1)} %constant_dynamic-update-slice_fusion, s32[]{:T(128)S(6)} %select_n.14), kind=kOutput, calls=%fused_computation.71 | convolution fusion | flops 2147483648 | bytes 11534340 | tf_op jit(solution)/shard_map/frk,fkn->frn/dot_general | solution.py:27
  310.5 8.1 %fusion.27 = f32[256,2048]{0,1:T(8,128)} fusion(bf16[1,2,256,2048]{2,3,1,0:T(8,128)(2,1)S(1)} %fusion.38, bf16[1,2,4096,2048]{3,2,1,0:T(8,128)(2,1)} %constant_dynamic-update-slice_fusion, s32[]{:T(128)S(6)} %add.94, s32[]{:T(128)S(6)} %select_n.14), kind=kOutput, calls=%fused_computation.72 | convolution fusion | flops 2147483648 | bytes 11534344 | tf_op jit(solution)/shard_map/frk,fkn->frn/dot_general | solution.py:24
  320.5 7.8 %fusion.16 = f32[1,1,256,2048]{2,3,1,0:T(8,128)S(1)} fusion(f32[256,2048]{0,1:T(8,128)} %fusion.26, bf16[1,2,256,2048]{2,3,1,0:T(8,128)(2,1)} %copy-done.25, bf16[1,2,4096,2048]{3,2,1,0:T(8,128)(2,1)} %constant_dynamic-update-slice_fusion, s32[]{:T(128)S(6)} %add.94, s32[]{:T(128)S(6)} %select_n.14), kind=kOutput, calls=%fused_computation.48 | convolution fusion | flops 2148007936 | bytes 13631496 | tf_op jit(solution)/shard_map/frk,fkn->frn/dot_general | solution.py:25
  328.3 7.3 %fusion.17 = f32[1,1,256,2048]{2,3,1,0:T(8,128)S(1)} fusion(f32[256,2048]{0,1:T(8,128)S(1)} %copy-done.27, bf16[1,2,256,2048]{2,3,1,0:T(8,128)(2,1)S(1)} %copy-done.26, bf16[1,2,4096,2048]{3,2,1,0:T(8,128)(2,1)} %constant_dynamic-update-slice_fusion, s32[]{:T(128)S(6)} %select_n.14), kind=kOutput, calls=%fused_computation.50 | convolution fusion | flops 2148007936 | bytes 13631492 | tf_op jit(solution)/shard_map/frk,fkn->frn/dot_general | solution.py:22
  335.7 1.7 fusion.42
  337.4 7.3 %fusion.28 = f32[256,2048]{0,1:T(8,128)S(1)} fusion(bf16[1,2,256,2048]{2,3,1,0:T(8,128)(2,1)S(1)} %get-tuple-element.32, bf16[1,2,4096,2048]{3,2,1,0:T(8,128)(2,1)} %constant_dynamic-update-slice_fusion, s32[]{:T(128)S(6)} %add.94, s32[]{:T(128)S(6)} %select_n.14), kind=kOutput, calls=%fused_computation.73 | convolution fusion | flops 2147483648 | bytes 11534344 | tf_op jit(solution)/shard_map/frk,fnk->frn/dot_general | solution.py:37
  344.6 5.7 %fusion.29 = f32[256,2048]{0,1:T(8,128)S(1)} fusion(bf16[1,2,256,2048]{2,3,1,0:T(8,128)(2,1)S(1)} %get-tuple-element.32, bf16[1,2,4096,2048]{3,2,1,0:T(8,128)(2,1)} %constant_dynamic-update-slice_fusion, s32[]{:T(128)S(6)} %add.94, s32[]{:T(128)S(6)} %select_n.14), kind=kOutput, calls=%fused_computation.74 | convolution fusion | flops 2147483648 | bytes 11534344 | tf_op jit(solution)/shard_map/frk,fnk->frn/dot_general | solution.py:34
  350.4 5.9 %fusion.12 = f32[1,1,256,2048]{2,3,1,0:T(8,128)S(1)} fusion(f32[256,2048]{0,1:T(8,128)S(1)} %fusion.28, bf16[1,2,256,2048]{2,3,1,0:T(8,128)(2,1)S(1)} %get-tuple-element.32, bf16[1,2,4096,2048]{3,2,1,0:T(8,128)(2,1)} %constant_dynamic-update-slice_fusion, s32[]{:T(128)S(6)} %select_n.14), kind=kOutput, calls=%fused_computation.40 | convolution fusion | flops 2148007936 | bytes 13631492 | tf_op jit(solution)/shard_map/frk,fnk->frn/dot_general | solution.py:35
  356.3 6.5 %fusion.13 = f32[1,1,256,2048]{2,3,1,0:T(8,128)S(1)} fusion(f32[256,2048]{0,1:T(8,128)S(1)} %fusion.29, bf16[1,2,256,2048]{2,3,1,0:T(8,128)(2,1)S(1)} %get-tuple-element.32, bf16[1,2,4096,2048]{3,2,1,0:T(8,128)(2,1)} %constant_dynamic-update-slice_fusion, s32[]{:T(128)S(6)} %select_n.14), kind=kOutput, calls=%fused_computation.42 | convolution fusion | flops 2148007936 | bytes 13631492 | tf_op jit(solution)/shard_map/frk,fnk->frn/dot_general | solution.py:32
  362.8 4.4 multiply_reduce_fusion.5
  367.2 38.9 %all-reduce.1 = (f32[]{:T(128)}, f32[]{:T(128)}, f32[]{:T(128)}, f32[]{:T(128)}) all-reduce(f32[]{:T(128)} %get-tuple-element.13, f32[]{:T(128)} %get-tuple-element.7, f32[]{:T(128)} %get-tuple-element.6, f32[]{:T(128)} %get-tuple-element.12), channel_id=1, replica_groups=mesh['freq'=4,'row'=8] {'freq','row'}, use_global_device_ids=true, to_apply=%region_8.9 | all-reduce | flops 4 | bytes 32 | tf_op jit(solution)/shard_map/psum | solution.py:50
  406.7 7.4 %fusion.41 = (bf16[1,2,256,2048]{2,3,1,0:T(8,128)(2,1)S(1)}, f32[1,2,256,2048]{2,3,1,0:T(8,128)}) fusion(f32[1,2,256,2048]{2,3,1,0:T(8,128)} %get-tuple-element.31, f32[]{:T(128)S(6)} %sqrt.26, f32[1,2,256,2048]{2,3,1,0:T(8,128)} %copy-done, f32[1,1,256,2048]{2,3,1,0:T(8,128)} %copy-done.21, f32[1,1,256,2048]{2,3,1,0:T(8,128)} %copy-done.22), kind=kLoop, calls=%fused_computation.101 | loop fusion | flops 7340032 | bytes 18874372 | tf_op jit(solution)/shard_map/convert_element_type | solution.py:73
  414.1 8.1 %fusion.30 = f32[256,2048]{0,1:T(8,128)} fusion(bf16[1,2,256,2048]{2,3,1,0:T(8,128)(2,1)S(1)} %get-tuple-element.29, bf16[1,2,4096,2048]{3,2,1,0:T(8,128)(2,1)} %constant_dynamic-update-slice_fusion, s32[]{:T(128)S(6)} %select_n.14), kind=kOutput, calls=%fused_computation.75 | convolution fusion | flops 2147483648 | bytes 11534340 | tf_op jit(solution)/shard_map/frk,fkn->frn/dot_general | solution.py:27
  422.2 8.1 %fusion.31 = f32[256,2048]{0,1:T(8,128)} fusion(bf16[1,2,256,2048]{2,3,1,0:T(8,128)(2,1)S(1)} %get-tuple-element.29, bf16[1,2,4096,2048]{3,2,1,0:T(8,128)(2,1)} %constant_dynamic-update-slice_fusion, s32[]{:T(128)S(6)} %add.94, s32[]{:T(128)S(6)} %select_n.14), kind=kOutput, calls=%fused_computation.76 | convolution fusion | flops 2147483648 | bytes 11534344 | tf_op jit(solution)/shard_map/frk,fkn->frn/dot_general | solution.py:24
  432.3 7.5 %fusion.14 = f32[1,1,256,2048]{2,3,1,0:T(8,128)S(1)} fusion(f32[256,2048]{0,1:T(8,128)} %fusion.30, bf16[1,2,256,2048]{2,3,1,0:T(8,128)(2,1)S(1)} %get-tuple-element.29, bf16[1,2,4096,2048]{3,2,1,0:T(8,128)(2,1)} %constant_dynamic-update-slice_fusion, s32[]{:T(128)S(6)} %add.94, s32[]{:T(128)S(6)} %select_n.14), kind=kOutput, calls=%fused_computation.44 | convolution fusion | flops 2148007936 | bytes 13631496 | tf_op jit(solution)/shard_map/frk,fkn->frn/dot_general | solution.py:25
  439.8 7.1 %fusion.15 = f32[1,1,256,2048]{2,3,1,0:T(8,128)S(1)} fusion(f32[256,2048]{0,1:T(8,128)S(1)} %copy-done.28, bf16[1,2,256,2048]{2,3,1,0:T(8,128)(2,1)S(1)} %get-tuple-element.29, bf16[1,2,4096,2048]{3,2,1,0:T(8,128)(2,1)} %constant_dynamic-update-slice_fusion, s32[]{:T(128)S(6)} %select_n.14), kind=kOutput, calls=%fused_computation.46 | convolution fusion | flops 2148007936 | bytes 13631492 | tf_op jit(solution)/shard_map/frk,fkn->frn/dot_general | solution.py:22
  447.0 2.5 fusion.39
  449.5 7.8 %fusion.32 = f32[256,2048]{0,1:T(8,128)} fusion(bf16[1,2,256,2048]{2,3,1,0:T(8,128)(2,1)S(1)} %get-tuple-element.27, bf16[1,2,4096,2048]{3,2,1,0:T(8,128)(2,1)} %constant_dynamic-update-slice_fusion, s32[]{:T(128)S(6)} %add.94, s32[]{:T(128)S(6)} %select_n.14), kind=kOutput, calls=%fused_computation.77 | convolution fusion | flops 2147483648 | bytes 11534344 | tf_op jit(solution)/shard_map/frk,fnk->frn/dot_general | solution.py:37
  457.3 7.1 %fusion.33 = f32[256,2048]{0,1:T(8,128)} fusion(bf16[1,2,256,2048]{2,3,1,0:T(8,128)(2,1)S(1)} %get-tuple-element.27, bf16[1,2,4096,2048]{3,2,1,0:T(8,128)(2,1)} %constant_dynamic-update-slice_fusion, s32[]{:T(128)S(6)} %add.94, s32[]{:T(128)S(6)} %select_n.14), kind=kOutput, calls=%fused_computation.78 | convolution fusion | flops 2147483648 | bytes 11534344 | tf_op jit(solution)/shard_map/frk,fnk->frn/dot_general | solution.py:34
  464.5 6.8 %fusion.10 = f32[1,1,256,2048]{2,3,1,0:T(8,128)S(1)} fusion(f32[256,2048]{0,1:T(8,128)} %fusion.32, bf16[1,2,256,2048]{2,3,1,0:T(8,128)(2,1)} %copy-done.23, bf16[1,2,4096,2048]{3,2,1,0:T(8,128)(2,1)} %constant_dynamic-update-slice_fusion, s32[]{:T(128)S(6)} %select_n.14), kind=kOutput, calls=%fused_computation.36 | convolution fusion | flops 2148007936 | bytes 13631492 | tf_op jit(solution)/shard_map/frk,fnk->frn/dot_general | solution.py:35
  471.4 6.1 %fusion.11 = f32[1,1,256,2048]{2,3,1,0:T(8,128)S(1)} fusion(f32[256,2048]{0,1:T(8,128)S(1)} %copy-done.29, bf16[1,2,256,2048]{2,3,1,0:T(8,128)(2,1)S(1)} %copy-done.24, bf16[1,2,4096,2048]{3,2,1,0:T(8,128)(2,1)} %constant_dynamic-update-slice_fusion, s32[]{:T(128)S(6)} %select_n.14), kind=kOutput, calls=%fused_computation.38 | convolution fusion | flops 2148007936 | bytes 13631492 | tf_op jit(solution)/shard_map/frk,fnk->frn/dot_general | solution.py:32
  477.5 2.5 multiply_reduce_fusion.1
  479.9 42.1 %all-reduce = (f32[]{:T(128)}, f32[]{:T(128)}, f32[]{:T(128)}, f32[]{:T(128)}) all-reduce(f32[]{:T(128)} %get-tuple-element.11, f32[]{:T(128)} %get-tuple-element.5, f32[]{:T(128)} %get-tuple-element.4, f32[]{:T(128)} %get-tuple-element.10), channel_id=1, replica_groups=mesh['freq'=4,'row'=8] {'freq','row'}, use_global_device_ids=true, to_apply=%region_16.17 | all-reduce | flops 4 | bytes 32 | tf_op jit(solution)/shard_map/psum | solution.py:50
  524.9 8.5 %multiply_subtract_fusion = (f32[1,2,256,2048]{2,3,1,0:T(8,128)}, f32[1,2,256,2048]{2,3,1,0:T(8,128)}) fusion(f32[1,2,256,2048]{2,3,1,0:T(8,128)} %get-tuple-element.31, f32[]{:T(128)S(6)} %div.111, f32[]{:T(128)S(6)} %sqrt.31, f32[]{:T(128)S(6)} %sqrt.29, f32[]{:T(128)S(6)} %div.104, f32[1,2,256,2048]{2,3,1,0:T(8,128)} %get-tuple-element.28, ...), kind=kLoop, calls=%fused_computation.20 | loop fusion | flops 15728640 | bytes 25165852 | tf_op jit(solution)/shard_map/sub | solution.py:88
  533.5 5.3 copy.20
  538.8 5.3 copy.21
  (76 shorter events, 20.4 us)
Async XLA Ops:
  0.6 25.7 %collective-permute-start = (bf16[1,2,256,2048]{3,2,1,0:T(8,128)(2,1)}, bf16[1,2,256,2048]{3,2,1,0:T(8,128)(2,1)S(1)}, u32[]{:S(2)}, u32[]{:S(2)}) collective-permute-start(bf16[1,2,256,2048]{3,2,1,0:T(8,128)(2,1)} %param.1), channel_id=1, source_target_pairs={{0,1},{1,2},{2,3},{3,4},{4,5},{5,6},{6,7},{7,0},{8,9},{9,10},{10,1... | collective-permute-start | bytes 6291464 | tf_op jit(solution)/shard_map/ppermute | solution.py:15
  26.4 1.3 copy-start.10
  27.7 25.5 %collective-permute-start.1 = (bf16[1,2,256,2048]{3,2,1,0:T(8,128)(2,1)S(1)}, bf16[1,2,256,2048]{3,2,1,0:T(8,128)(2,1)S(1)}, u32[]{:S(2)}, u32[]{:S(2)}) collective-permute-start(bf16[1,2,256,2048]{3,2,1,0:T(8,128)(2,1)S(1)} %collective-permute-done), channel_id=1, source_target_pairs={{0,1},{1,2},{2,3},{3,4},{4,5},{5,6},{6,7},{7,0},{8,9},{9,10},{10,1... | collective-permute-start | bytes 6291464 | tf_op jit(solution)/shard_map/ppermute | solution.py:15
  53.1 1.3 copy-start.12
  54.4 25.5 %collective-permute-start.2 = (bf16[1,2,256,2048]{3,2,1,0:T(8,128)(2,1)S(1)}, bf16[1,2,256,2048]{3,2,1,0:T(8,128)(2,1)S(1)}, u32[]{:S(2)}, u32[]{:S(2)}) collective-permute-start(bf16[1,2,256,2048]{3,2,1,0:T(8,128)(2,1)S(1)} %collective-permute-done.1), channel_id=1, source_target_pairs={{0,1},{1,2},{2,3},{3,4},{4,5},{5,6},{6,7},{7,0},{8,9},{9,10},{10,1... | collective-permute-start | bytes 6291464 | tf_op jit(solution)/shard_map/ppermute | solution.py:15
  79.9 1.3 copy-start.14
  81.2 25.5 %collective-permute-start.3 = (bf16[1,2,256,2048]{3,2,1,0:T(8,128)(2,1)S(1)}, bf16[1,2,256,2048]{3,2,1,0:T(8,128)(2,1)S(1)}, u32[]{:S(2)}, u32[]{:S(2)}) collective-permute-start(bf16[1,2,256,2048]{3,2,1,0:T(8,128)(2,1)S(1)} %collective-permute-done.2), channel_id=1, source_target_pairs={{0,1},{1,2},{2,3},{3,4},{4,5},{5,6},{6,7},{7,0},{8,9},{9,10},{10,1... | collective-permute-start | bytes 6291464 | tf_op jit(solution)/shard_map/ppermute | solution.py:15
  106.7 1.3 copy-start.16
  108.0 25.5 %collective-permute-start.4 = (bf16[1,2,256,2048]{3,2,1,0:T(8,128)(2,1)S(1)}, bf16[1,2,256,2048]{3,2,1,0:T(8,128)(2,1)S(1)}, u32[]{:S(2)}, u32[]{:S(2)}) collective-permute-start(bf16[1,2,256,2048]{3,2,1,0:T(8,128)(2,1)S(1)} %collective-permute-done.3), channel_id=1, source_target_pairs={{0,1},{1,2},{2,3},{3,4},{4,5},{5,6},{6,7},{7,0},{8,9},{9,10},{10,1... | collective-permute-start | bytes 6291464 | tf_op jit(solution)/shard_map/ppermute | solution.py:15
  133.5 1.3 copy-start.18
  134.8 25.6 %collective-permute-start.5 = (bf16[1,2,256,2048]{3,2,1,0:T(8,128)(2,1)S(1)}, bf16[1,2,256,2048]{3,2,1,0:T(8,128)(2,1)}, u32[]{:S(2)}, u32[]{:S(2)}) collective-permute-start(bf16[1,2,256,2048]{3,2,1,0:T(8,128)(2,1)S(1)} %collective-permute-done.4), channel_id=1, source_target_pairs={{0,1},{1,2},{2,3},{3,4},{4,5},{5,6},{6,7},{7,0},{8,9},{9,10},{10,1... | collective-permute-start | bytes 6291464 | tf_op jit(solution)/shard_map/ppermute | solution.py:15
  160.4 25.8 %collective-permute-start.6 = (bf16[1,2,256,2048]{3,2,1,0:T(8,128)(2,1)}, bf16[1,2,256,2048]{3,2,1,0:T(8,128)(2,1)}, u32[]{:S(2)}, u32[]{:S(2)}) collective-permute-start(bf16[1,2,256,2048]{3,2,1,0:T(8,128)(2,1)} %collective-permute-done.5), channel_id=1, source_target_pairs={{0,1},{1,2},{2,3},{3,4},{4,5},{5,6},{6,7},{7,0},{8,9},{9,10},{10,1... | collective-permute-start | bytes 6291464 | tf_op jit(solution)/shard_map/ppermute | solution.py:15
  163.2 29.6 %copy-start.19 = (bf16[1,2,256,2048]{3,2,1,0:T(8,128)(2,1)S(1)}, bf16[1,2,256,2048]{3,2,1,0:T(8,128)(2,1)}, u32[]{:S(2)}) copy-start(bf16[1,2,256,2048]{3,2,1,0:T(8,128)(2,1)} %copy-done.18) | copy-start | bytes 6291460
  189.3 5.0 copy-start.17
  192.8 3.0 copy-start.15
  194.4 3.0 copy-start.13
  195.8 3.1 copy-start.11
  197.4 3.1 copy-start.9
  235.5 6.8 %copy-start.5 = (f32[1,1,256,2048]{2,3,1,0:T(8,128)}, f32[1,1,256,2048]{2,3,1,0:T(8,128)S(1)}, u32[]{:S(2)}) copy-start(f32[1,1,256,2048]{2,3,1,0:T(8,128)S(1)} %fusion.18) | copy-start | bytes 6291460
  242.3 2.1 copy-start.7
  301.6 8.8 %copy-start.25 = (bf16[1,2,256,2048]{2,3,1,0:T(8,128)(2,1)}, bf16[1,2,256,2048]{2,3,1,0:T(8,128)(2,1)S(1)}, u32[]{:S(2)}) copy-start(bf16[1,2,256,2048]{2,3,1,0:T(8,128)(2,1)S(1)} %fusion.38) | copy-start | bytes 6291460
  320.5 7.8 %copy-start.26 = (bf16[1,2,256,2048]{2,3,1,0:T(8,128)(2,1)S(1)}, bf16[1,2,256,2048]{2,3,1,0:T(8,128)(2,1)}, u32[]{:S(2)}) copy-start(bf16[1,2,256,2048]{2,3,1,0:T(8,128)(2,1)} %copy-done.25) | copy-start | bytes 6291460
  320.5 7.8 %copy-start.27 = (f32[256,2048]{0,1:T(8,128)S(1)}, f32[256,2048]{0,1:T(8,128)}, u32[]{:S(2)}) copy-start(f32[256,2048]{0,1:T(8,128)} %fusion.27) | copy-start | bytes 6291460
  328.3 7.3 %copy-start.6 = (f32[1,1,256,2048]{2,3,1,0:T(8,128)S(1)}, f32[1,1,256,2048]{2,3,1,0:T(8,128)}, u32[]{:S(2)}) copy-start(f32[1,1,256,2048]{2,3,1,0:T(8,128)} %copy-done.5) | copy-start | bytes 6291460
  328.3 7.3 %copy-start.8 = (f32[1,1,256,2048]{2,3,1,0:T(8,128)S(1)}, f32[1,1,256,2048]{2,3,1,0:T(8,128)}, u32[]{:S(2)}) copy-start(f32[1,1,256,2048]{2,3,1,0:T(8,128)} %copy-done.7) | copy-start | bytes 6291460
  337.4 25.5 %copy-start = (f32[1,2,256,2048]{2,3,1,0:T(8,128)}, f32[1,2,256,2048]{2,3,1,0:T(8,128)S(1)}, u32[]{:S(2)}) copy-start(f32[1,2,256,2048]{2,3,1,0:T(8,128)S(1)} %get-tuple-element.33) | copy-start | bytes 12582916
  356.3 6.5 %copy-start.21 = (f32[1,1,256,2048]{2,3,1,0:T(8,128)}, f32[1,1,256,2048]{2,3,1,0:T(8,128)S(1)}, u32[]{:S(2)}) copy-start(f32[1,1,256,2048]{2,3,1,0:T(8,128)S(1)} %fusion.12) | copy-start | bytes 6291460
  362.8 4.4 copy-start.22
  432.3 7.5 %copy-start.28 = (f32[256,2048]{0,1:T(8,128)S(1)}, f32[256,2048]{0,1:T(8,128)}, u32[]{:S(2)}) copy-start(f32[256,2048]{0,1:T(8,128)} %fusion.31) | copy-start | bytes 6291460
  439.8 7.2 %copy-start.1 = (f32[1,2,256,2048]{2,3,1,0:T(8,128)S(1)}, f32[1,2,256,2048]{2,3,1,0:T(8,128)}, u32[]{:S(2)}) copy-start(f32[1,2,256,2048]{2,3,1,0:T(8,128)} %copy-done) | copy-start | bytes 12582916
  439.8 7.2 %copy-start.2 = (f32[1,2,256,2048]{2,3,1,0:T(8,128)S(1)}, f32[1,2,256,2048]{2,3,1,0:T(8,128)}, u32[]{:S(2)}) copy-start(f32[1,2,256,2048]{2,3,1,0:T(8,128)} %get-tuple-element.30) | copy-start | bytes 12582916
  449.5 7.8 %copy-start.23 = (bf16[1,2,256,2048]{2,3,1,0:T(8,128)(2,1)}, bf16[1,2,256,2048]{2,3,1,0:T(8,128)(2,1)S(1)}, u32[]{:S(2)}) copy-start(bf16[1,2,256,2048]{2,3,1,0:T(8,128)(2,1)S(1)} %get-tuple-element.27) | copy-start | bytes 6291460
  464.5 6.8 %copy-start.24 = (bf16[1,2,256,2048]{2,3,1,0:T(8,128)(2,1)S(1)}, bf16[1,2,256,2048]{2,3,1,0:T(8,128)(2,1)}, u32[]{:S(2)}) copy-start(bf16[1,2,256,2048]{2,3,1,0:T(8,128)(2,1)} %copy-done.23) | copy-start | bytes 6291460
  464.5 6.8 %copy-start.29 = (f32[256,2048]{0,1:T(8,128)S(1)}, f32[256,2048]{0,1:T(8,128)}, u32[]{:S(2)}) copy-start(f32[256,2048]{0,1:T(8,128)} %fusion.33) | copy-start | bytes 6291460
  471.3 6.1 %copy-start.3 = (f32[1,2,256,2048]{2,3,1,0:T(8,128)S(1)}, f32[1,2,256,2048]{2,3,1,0:T(8,128)}, u32[]{:S(2)}) copy-start(f32[1,2,256,2048]{2,3,1,0:T(8,128)} %get-tuple-element.30) | copy-start | bytes 12582916
  471.3 6.1 %copy-start.4 = (f32[1,2,256,2048]{2,3,1,0:T(8,128)S(1)}, f32[1,2,256,2048]{2,3,1,0:T(8,128)}, u32[]{:S(2)}) copy-start(f32[1,2,256,2048]{2,3,1,0:T(8,128)} %get-tuple-element.28) | copy-start | bytes 12582916
  477.5 2.5 copy-start.20
